TPU v7x, 32 devices: a whole 2x2x4 slice. The times are simulated.
32 devices in a mesh: row: 8 (over z, x), col: 4 (over y, core).
Axes of the slice: x: 2, y: 2, z: 4, core: 2. Of those that a mesh axis runs over, the one named last changes fastest.
Arguments:
- amplitudes: float32 [200, 10, 10, 1024], P('row', None, None, 'col'), may hold values from -6 to 6
- old_blocks: int32 [8, 25], replicated, may hold values from 0 to 135, as said below
- old_counts: int32 [8], replicated, may hold values from 1 to 25, as said below
- new_phase: int32 [1], replicated, may hold values from 0 to 7
- fock: float32 [160, 160], P('row'), may hold values from -0.5 to 0.5
Outputs:
- contracted: float32 [16, 10, 160, 1024], P('row', None, None, 'col')
Inputs may be any that keep to these rules, and one draw needn't show every extreme that they name: `old_blocks`: over the live slots of all row devices every tile pair id 0 to 135 stands exactly once; ids in slots that are not live are arbitrary. For every residue r mod 8, at most 8 live blocks of one row device hold a tile whose index is r mod 8, and some device reaches 8 for some r. `old_counts`: the counts sum to 136; some device has exactly 25.
All inputs are finite; a program needn't handle non-finite values.
Results may differ from a plain program's by a relative error of at most 0.00007.
Values sent between devices are 32-bit elements; how exact they have to be, the bound alone decides.
No kernel may reach another device: no remote copies, remote signals or barrier semaphores. Data moves between devices by JAX's collectives and lax.ppermute only.
A program may use at most 128 MiB of HBM per device.

v0:
```python
import jax
import jax.numpy as jnp
import numpy as np
from jax import lax
from jax.sharding import PartitionSpec as P

NT = 16


def pair_table():
    table = np.zeros((NT, NT), np.int32)
    first_tile = np.zeros((NT * (NT + 1) // 2,), np.int32)
    second_tile = np.zeros((NT * (NT + 1) // 2,), np.int32)
    for first in range(NT):
        for second in range(NT):
            low = min(first, second)
            high = max(first, second)
            ident = low * NT - low * (low - 1) // 2 + (high - low)
            table[first, second] = ident
            first_tile[ident] = low
            second_tile[ident] = high
    return (table, first_tile, second_tile)


def body(amplitudes, old_blocks, old_counts, new_phase, fock):
    nrows = lax.axis_size("row")
    myself = lax.axis_index("row")
    slots = amplitudes.shape[0]
    tile = amplitudes.shape[1]
    occ_dev = amplitudes.shape[3]
    width = fock.shape[1]
    per_dev = NT // nrows
    nblocks = NT * (NT + 1) // 2
    phase = new_phase[0]
    table, first_tile, second_tile = pair_table()
    live = jnp.arange(slots, dtype=jnp.int32)[None, :] < old_counts[:, None]
    flat = amplitudes.reshape(slots, tile * tile * occ_dev)
    fock_full = lax.all_gather(fock, "row", axis=0, tiled=True)
    match_ids = old_blocks.reshape(-1)
    match_live = live.reshape(-1)
    my_ids = lax.dynamic_slice_in_dim(old_blocks, myself, 1, 0)[0]
    my_live = lax.dynamic_slice_in_dim(live, myself, 1, 0)[0]
    owner_low = (jnp.asarray(first_tile)[my_ids] + phase) % nrows
    owner_high = (jnp.asarray(second_tile)[my_ids] + phase) % nrows
    target = jnp.arange(nrows, dtype=jnp.int32)[:, None]
    sending = ((owner_low[None, :] == target) | (owner_high[None, :] == target)) & my_live[None, :]
    capacity = per_dev * ((slots - 2) // 8 + 2)
    ordinal = jnp.cumsum(sending.astype(jnp.int32), axis=1) - 1
    packing = (
        ordinal[:, None, :] == jnp.arange(capacity, dtype=jnp.int32)[None, :, None]
    ) & sending[:, None, :]
    payload = jnp.einsum(
        "dcs,sp->dcp", packing.astype(jnp.float32), flat, precision=lax.Precision.HIGHEST
    )
    filled = jnp.any(packing, axis=2)
    sent_ids = jnp.sum(jnp.where(packing, my_ids[None, None, :], 0), axis=2)
    sent_ids = jnp.where(filled, sent_ids, nblocks)
    payload_in, ids_in = (
        lax.all_to_all(payload, "row", split_axis=0, concat_axis=0, tiled=True),
        lax.all_to_all(sent_ids, "row", split_axis=0, concat_axis=0, tiled=True),
    )
    received = payload_in
    match_ids = ids_in.reshape(-1)
    match_live = match_ids < nblocks
    received = received.reshape(-1, tile * tile * occ_dev)
    index = jnp.arange(tile, dtype=jnp.int32)
    results = []
    for within in range(per_dev):
        column_tile = (myself - phase) % nrows + within * nrows
        needed = jnp.asarray(table)[:, column_tile]
        picker = ((match_ids[None, :] == needed[:, None]) & match_live[None, :]).astype(jnp.float32)
        chosen = jnp.dot(picker, received, precision=lax.Precision.HIGHEST)
        chosen = chosen.reshape(NT, tile, tile, occ_dev)
        c_global = jnp.arange(NT, dtype=jnp.int32)[:, None, None] * tile + index[None, :, None]
        b_global = column_tile * tile + index[None, None, :]
        below = (c_global < b_global)[:, :, :, None]
        above = (c_global > b_global)[:, :, :, None]
        dense = jnp.where(below, chosen, jnp.where(above, -jnp.swapaxes(chosen, 1, 2), 0.0))
        dense = dense.reshape(width, tile, occ_dev)
        outcome = jnp.einsum("ac,cbj->baj", fock_full, dense, precision=lax.Precision.HIGHEST)
        results.append(outcome)
    return jnp.stack(results, 0)


def solution(mesh):
    return jax.shard_map(
        body,
        mesh=mesh,
        in_specs=(P("row", None, None, "col"), P(), P(), P(), P("row", None)),
        out_specs=P("row", None, None, "col"),
        check_vma=False,
    )
```

profile of v0, /device:TPU:0, one launch (start us, length us, event | category | flops | bytes accessed | tf_op | source)
XLA Modules:
  0.0 239.0 jit_solution(3944722288822886608)
XLA Ops:
  0.0 0.7 fusion.30
  0.7 0.7 fusion.31
  1.4 1.4 gather_fusion
  2.8 1.4 gather_fusion.1
  4.8 0.7 iota_compare_fusion.1
  5.6 0.2 reduce_window_sum.11
  5.8 0.2 fusion.9
  6.0 0.2 select_reduce_fusion
  6.2 0.6 broadcast_select_fusion
  6.8 7.3 %all-to-all-start = ((s32[8,1,8]{2,1,0:T(1,128)}), s32[8,1,8]{2,1,0:T(1,128)S(1)}, u32[]{:S(2)}, u32[]{:S(2)}) async-start(s32[8,1,8]{2,1,0:T(1,128)} %bitcast.6), calls=%async_computation | async-start | bytes 8192 | tf_op jit(solution)/shard_map/all_to_all | solution.py:60
  14.1 5.4 %copy.19 = f32[25,10,10,256]{3,2,1,0:T(8,128)} copy(f32[25,10,10,256]{3,0,2,1:T(8,128)} %param.8) | data formatting | bytes 5120000 | tf_op args[0]
  19.5 3.2 %reshape.256 = f32[25,25600,1]{1,0,2:T(8,128)S(1)} reshape(f32[25,10,10,256]{3,2,1,0:T(8,128)} %copy.19) | data formatting | bytes 5120000 | tf_op jit(solution)/shard_map/reshape | solution.py:37
  22.7 4.6 %fusion.7 = f32[8,8,25600]{2,1,0:T(8,128)} fusion(f32[25,25600,1]{1,0,2:T(8,128)S(1)} %reshape.256, s32[8,25]{1,0:T(8,128)S(1)} %broadcast_add_fusion, pred[8,25]{1,0:T(8,128)(4,1)S(1)} %get-tuple-element.6), kind=kOutput, calls=%fused_computation.22 | convolution fusion | flops 491523200 | bytes 9114600 | tf_op jit(solution)/shard_map/dcs,sp->dcp/dot_general | solution.py:52
  27.4 6.1 %all-to-all-start.1 = ((f32[8,8,25600]{2,1,0:T(8,128)}), f32[8,8,25600]{2,1,0:T(8,128)}, u32[]{:S(2)}, u32[]{:S(2)}) async-start(f32[8,8,25600]{2,1,0:T(8,128)} %fusion.7), calls=%async_computation.1 | async-start | bytes 13107200 | tf_op jit(solution)/shard_map/all_to_all | solution.py:59
  33.5 163.5 %all-gather = f32[8,20,160]{2,1,0:T(8,128)S(1)} all-gather(f32[1,20,160]{2,1,0:T(8,128)S(1)} %bitcast.59), channel_id=1, replica_groups=mesh['row'=8,'col'=4] {'row'}, dimensions={0}, use_global_device_ids=true | all-gather | bytes 115200 | tf_op jit(solution)/shard_map/all_gather | solution.py:38
  197.0 0.7 fusion.26
  197.7 0.1 broadcast_compare_fusion.3
  197.9 0.5 broadcast.232
  198.4 0.7 reduce.3
  199.0 0.1 eq.100
  199.1 8.8 %dot_general.21 = f32[10,10,256,64]{2,1,0,3:T(8,128)} reshape(f32[25600,64]{0,1:T(8,128)} %bitcast.11) | data formatting | bytes 13107200 | tf_op jit(solution)/shard_map/dot_general | solution.py:72
  208.0 9.2 %fusion.2 = f32[16,10,10,256]{3,0,2,1:T(8,128)S(1)} fusion(f32[10,10,256,64]{2,1,0,3:T(8,128)} %dot_general.21, s32[64]{0:T(128)S(1)} %eq.100, s32[16]{0:T(128)S(1)} %get-tuple-element.13, pred[64]{0:T(512)(128)(4,1)S(1)} %broadcast_compare_fusion.4), kind=kOutput, calls=%fused_computation.4 | convolution fusion | flops 314574848 | bytes 8192384 | tf_op jit(solution)/shard_map/dot_general | solution.py:72
  217.2 0.6 fusion.5
  217.8 1.1 copy.22
  218.8 1.3 reshape.236
  220.1 9.2 %fusion = f32[16,10,10,256]{3,0,2,1:T(8,128)S(1)} fusion(f32[10,10,256,64]{2,1,0,3:T(8,128)} %dot_general.21, s32[64]{0:T(128)S(1)} %eq.100, s32[16]{0:T(128)S(1)} %get-tuple-element.14, pred[64]{0:T(512)(128)(4,1)S(1)} %broadcast_compare_fusion.4), kind=kOutput, calls=%fused_computation.2 | convolution fusion | flops 314574848 | bytes 8192384 | tf_op jit(solution)/shard_map/dot_general | solution.py:72
  229.3 0.6 fusion.4
  229.9 1.1 copy.25
  231.0 1.3 reshape.237
  232.3 3.2 %convolution_bitcast_fusion.1 = f32[1,10,160,256]{3,2,1,0:T(8,128)S(1)} fusion(f32[160,10,256]{2,0,1:T(8,128)} %reshape.236, f32[160,160,1]{1,0,2:T(8,128)S(1)} %reshape.258), kind=kOutput, calls=%fused_computation.14 | convolution fusion | flops 786432000 | bytes 3379200 | tf_op jit(solution)/shard_map/ac,cbj->baj/dot_general | solution.py:80
  235.4 1.6 convolution_bitcast_fusion
  237.0 1.9 pad_maximum_fusion
  (16 shorter events, 0.1 us)
Async XLA Ops:
  6.8 20.5 %all-to-all-start = ((s32[8,1,8]{2,1,0:T(1,128)}), s32[8,1,8]{2,1,0:T(1,128)S(1)}, u32[]{:S(2)}, u32[]{:S(2)}) async-start(s32[8,1,8]{2,1,0:T(1,128)} %bitcast.6), calls=%async_computation | async-start | bytes 8192 | tf_op jit(solution)/shard_map/all_to_all | solution.py:60
  27.3 6.1 %copy-start.1 = (f32[20,160]{1,0:T(8,128)S(1)}, f32[20,160]{1,0:T(8,128)}, u32[]{:S(2)}) copy-start(f32[20,160]{1,0:T(8,128)} %param.12) | copy-start | bytes 38404
  27.4 171.8 %all-to-all-start.1 = ((f32[8,8,25600]{2,1,0:T(8,128)}), f32[8,8,25600]{2,1,0:T(8,128)}, u32[]{:S(2)}, u32[]{:S(2)}) async-start(f32[8,8,25600]{2,1,0:T(8,128)} %fusion.7), calls=%async_computation.1 | async-start | bytes 13107200 | tf_op jit(solution)/shard_map/all_to_all | solution.py:59
  232.3 3.2 %copy-start = (f32[160,10,256]{2,0,1:T(8,128)S(1)}, f32[160,10,256]{2,0,1:T(8,128)}, u32[]{:S(2)}) copy-start(f32[160,10,256]{2,0,1:T(8,128)} %reshape.237) | copy-start | bytes 4915204
where the time goes:
time: 240 us; the launch traced here: 239 us
  blocking collectives  163 us (68%)
  matrix products  27.7 us (12%)
  local copies, waits for them, and re-layouts  27 us (11%)
  starting transfers between devices  13.4 us (6%)
  other arithmetic  6.61 us (3%)
    all_gather x1, blocking collectives, body(): fock_full = lax.all_gather(fock, 'row', axis=0, tiled=True)  163 us
    dot_general x2, matrix products, body(): chosen = jnp.dot(picker, received, precision=lax.Precision.HIGHEST)  18.3 us
    dot_general x1, local copies, waits for them, and re-layouts, body(): chosen = jnp.dot(picker, received, precision=lax.Precision.HIGHEST)  8.85 us
    all_to_all x1, starting transfers between devices, body(): lax.all_to_all(sent_ids, 'row', split_axis=0, concat_axis=0, tiled=True)  7.28 us
    all_to_all x1, starting transfers between devices, body(): lax.all_to_all(payload, 'row', split_axis=0, concat_axis=0, tiled=True)  6.13 us
    unnamed x6, local copies, waits for them, and re-layouts  5.44 us
  transfers between devices with their start and end apart: 2, of which 0 were waited for; matrix products, arithmetic and copies ran while one was open for 6% of the time, Pallas kernels for 0%

commit v1 on v0

--- a/solution.py
+++ b/solution.py
@@ -5,6 +5,18 @@
 from jax.sharding import PartitionSpec as P
 
 NT = 16
+
+
+def gather_by_bits(x, axis, dim):
+    ways, here = (lax.axis_size(axis), lax.axis_index(axis))
+    grown, reach = (x, 1)
+    while reach < ways:
+        theirs = lax.ppermute(grown, axis, [(d, d ^ reach) for d in range(ways)])
+        mine_first = jnp.concatenate([grown, theirs], axis=dim)
+        theirs_first = jnp.concatenate([theirs, grown], axis=dim)
+        grown = jnp.where(here & reach == 0, mine_first, theirs_first)
+        reach = 2 * reach
+    return grown
 
 
 def pair_table():
@@ -35,7 +47,7 @@
     table, first_tile, second_tile = pair_table()
     live = jnp.arange(slots, dtype=jnp.int32)[None, :] < old_counts[:, None]
     flat = amplitudes.reshape(slots, tile * tile * occ_dev)
-    fock_full = lax.all_gather(fock, "row", axis=0, tiled=True)
+    fock_full = gather_by_bits(fock, "row", 0)
     match_ids = old_blocks.reshape(-1)
     match_live = live.reshape(-1)
     my_ids = lax.dynamic_slice_in_dim(old_blocks, myself, 1, 0)[0]

time: 240 us -> 222 us (0.925)
  blocking collectives: 163 us -> 0 us
  waiting for transfers between devices: 0.01 us -> 136 us
  starting transfers between devices: 13.4 us -> 21 us
    all_gather x1 -> x0, blocking collectives: 163 us -> none  [body(): fock_full = lax.all_gather(fock, 'row', axis=0, tiled=True)]
    ppermute x0 -> x3, waiting for transfers between devices: none -> 101 us  [gather_by_bits(): theirs = lax.ppermute(grown, axis, [(d, d ^ reach) for d in range(ways)])]
    all_to_all x1, waiting for transfers between devices: 0.01 us -> 35.3 us  [body(): lax.all_to_all(payload, 'row', split_axis=0, concat_axis=0, tiled=True)]
    ppermute x0 -> x3, starting transfers between devices: none -> 7.56 us  [gather_by_bits(): theirs = lax.ppermute(grown, axis, [(d, d ^ reach) for d in range(ways)])]
    unnamed x6 -> x5, local copies, waits for them, and re-layouts: 5.44 us -> 5.42 us
  transfers between devices with their start and end apart: 2 -> 5, of which waited for: 0 -> 3; matrix products, arithmetic and copies ran while one was open for 6% -> 23% of each run, Pallas kernels for 0% -> 0%
where the time goes in v1:
time: 222 us
  waiting for transfers between devices  136 us (61%)
  local copies, waits for them, and re-layouts  28.4 us (13%)
  matrix products  27.7 us (12%)
  starting transfers between devices  21 us (9%)
  other arithmetic  7.51 us (3%)
    ppermute x3, waiting for transfers between devices, gather_by_bits(): theirs = lax.ppermute(grown, axis, [(d, d ^ reach) for d in range(ways)])  101 us
    all_to_all x1, waiting for transfers between devices, body(): lax.all_to_all(payload, 'row', split_axis=0, concat_axis=0, tiled=True)  35.3 us
    dot_general x2, matrix products, body(): chosen = jnp.dot(picker, received, precision=lax.Precision.HIGHEST)  18.3 us
    dot_general x1, local copies, waits for them, and re-layouts, body(): chosen = jnp.dot(picker, received, precision=lax.Precision.HIGHEST)  8.82 us
    ppermute x3, starting transfers between devices, gather_by_bits(): theirs = lax.ppermute(grown, axis, [(d, d ^ reach) for d in range(ways)])  7.56 us
    all_to_all x1, starting transfers between devices, body(): lax.all_to_all(sent_ids, 'row', split_axis=0, concat_axis=0, tiled=True)  7.28 us
    all_to_all x1, starting transfers between devices, body(): lax.all_to_all(payload, 'row', split_axis=0, concat_axis=0, tiled=True)  6.13 us
    unnamed x5, local copies, waits for them, and re-layouts  5.42 us
  transfers between devices with their start and end apart: 5, of which 3 were waited for; matrix products, arithmetic and copies ran while one was open for 23% of the time, Pallas kernels for 0%

profile of v1, /device:TPU:0, one launch (start us, length us, event | category | flops | bytes accessed | tf_op | source)
XLA Modules:
  0.0 221.5 jit_solution(14902357993389569415)
XLA Ops:
  0.0 0.7 fusion.35
  0.7 0.7 fusion.36
  1.4 1.4 gather_fusion
  2.8 1.4 gather_fusion.1
  4.8 0.7 iota_compare_fusion.1
  6.2 0.6 broadcast_select_fusion
  6.8 7.3 %all-to-all-start = ((s32[8,1,8]{2,1,0:T(1,128)}), s32[8,1,8]{2,1,0:T(1,128)S(1)}, u32[]{:S(2)}, u32[]{:S(2)}) async-start(s32[8,1,8]{2,1,0:T(1,128)} %bitcast.6), calls=%async_computation | async-start | bytes 8192 | tf_op jit(solution)/shard_map/all_to_all | solution.py:72
  14.1 5.4 %copy.19 = f32[25,10,10,256]{3,2,1,0:T(8,128)} copy(f32[25,10,10,256]{3,0,2,1:T(8,128)} %param.8) | data formatting | bytes 5120000 | tf_op args[0]
  19.5 3.2 %reshape.254 = f32[25,25600,1]{1,0,2:T(8,128)S(1)} reshape(f32[25,10,10,256]{3,2,1,0:T(8,128)} %copy.19) | data formatting | bytes 5120000 | tf_op jit(solution)/shard_map/reshape | solution.py:49
  22.7 4.6 %fusion.12 = f32[8,8,25600]{2,1,0:T(8,128)} fusion(f32[25,25600,1]{1,0,2:T(8,128)S(1)} %reshape.254, s32[8,25]{1,0:T(8,128)S(1)} %broadcast_add_fusion, pred[8,25]{1,0:T(8,128)(4,1)S(1)} %get-tuple-element.6), kind=kOutput, calls=%fused_computation.28 | convolution fusion | flops 491523200 | bytes 9114600 | tf_op jit(solution)/shard_map/dcs,sp->dcp/dot_general | solution.py:64
  27.4 6.1 %all-to-all-start.1 = ((f32[8,8,25600]{2,1,0:T(8,128)}), f32[8,8,25600]{2,1,0:T(8,128)}, u32[]{:S(2)}, u32[]{:S(2)}) async-start(f32[8,8,25600]{2,1,0:T(8,128)} %fusion.12), calls=%async_computation.1 | async-start | bytes 13107200 | tf_op jit(solution)/shard_map/all_to_all | solution.py:71
  33.5 2.0 collective-permute-start
  35.7 0.7 fusion.31
  36.4 0.5 broadcast.232
  36.9 0.7 reduce.3
  37.6 48.8 %collective-permute-done = f32[20,160]{1,0:T(8,128)S(1)} collective-permute-done((f32[20,160]{1,0:T(8,128)S(1)}, f32[20,160]{1,0:T(8,128)S(1)}, u32[]{:S(2)}, u32[]{:S(2)}) %collective-permute-start) | collective-permute-done | bytes 12832 | tf_op jit(solution)/shard_map/ppermute | solution.py:14
  86.5 1.6 collective-permute-start.1
  88.1 52.0 %collective-permute-done.1 = f32[40,160]{1,0:T(8,128)S(1)} collective-permute-done((f32[40,160]{1,0:T(8,128)S(1)}, f32[40,160]{1,0:T(8,128)S(1)}, u32[]{:S(2)}, u32[]{:S(2)}) %collective-permute-start.1) | collective-permute-done | bytes 25632 | tf_op jit(solution)/shard_map/ppermute | solution.py:14
  140.2 3.9 %collective-permute-start.2 = (f32[80,160]{1,0:T(8,128)S(1)}, f32[80,160]{1,0:T(8,128)S(1)}, u32[]{:S(2)}, u32[]{:S(2)}) collective-permute-start(f32[80,160]{1,0:T(8,128)S(1)} %maximum_select_fusion.1), channel_id=1, source_target_pairs={{0,16},{4,20},{8,24},{12,28},{16,0},{20,4},{24,8},{28,12},{1,17},{... | collective-permute-start | bytes 153608 | tf_op jit(solution)/shard_map/ppermute | solution.py:14
  144.1 35.3 %all-to-all-done.1 = f32[8,8,25600]{2,1,0:T(8,128)} async-done(((f32[8,8,25600]{2,1,0:T(8,128)}), f32[8,8,25600]{2,1,0:T(8,128)}, u32[]{:S(2)}, u32[]{:S(2)}) %all-to-all-start.1) | async-done | bytes 6553632 | tf_op jit(solution)/shard_map/all_to_all | solution.py:71
  179.4 8.8 %dot_general.21 = f32[10,10,256,64]{2,1,0,3:T(8,128)} reshape(f32[25600,64]{0,1:T(8,128)} %bitcast.11) | data formatting | bytes 13107200 | tf_op jit(solution)/shard_map/dot_general | solution.py:84
  188.2 9.2 %fusion.2 = f32[16,10,10,256]{3,0,2,1:T(8,128)S(1)} fusion(f32[10,10,256,64]{2,1,0,3:T(8,128)} %dot_general.21, s32[64]{0:T(128)S(1)} %eq.109, s32[16]{0:T(128)S(1)} %get-tuple-element.13, pred[64]{0:T(512)(128)(4,1)S(1)} %broadcast_compare_fusion.4), kind=kOutput, calls=%fused_computation.4 | convolution fusion | flops 314574848 | bytes 8192384 | tf_op jit(solution)/shard_map/dot_general | solution.py:84
  197.4 9.2 %fusion = f32[16,10,10,256]{3,0,2,1:T(8,128)S(1)} fusion(f32[10,10,256,64]{2,1,0,3:T(8,128)} %dot_general.21, s32[64]{0:T(128)S(1)} %eq.109, s32[16]{0:T(128)S(1)} %get-tuple-element.14, pred[64]{0:T(512)(128)(4,1)S(1)} %broadcast_compare_fusion.4), kind=kOutput, calls=%fused_computation.2 | convolution fusion | flops 314574848 | bytes 8192384 | tf_op jit(solution)/shard_map/dot_general | solution.py:84
  206.6 0.6 fusion.5
  207.2 1.5 fusion.4
  208.7 1.1 copy.22
  209.7 1.3 reshape.236
  211.0 2.5 %copy.25 = f32[16,10,10,256]{3,1,0,2:T(8,128)S(1)} copy(f32[16,10,10,256]{3,0,2,1:T(8,128)} %fusion.4) | data formatting | bytes 3276800 | tf_op jit(solution)/shard_map/jit(_where)/select_n | solution.py:90
  213.5 1.3 reshape.237
  214.8 3.2 %convolution_bitcast_fusion.1 = f32[1,10,160,256]{3,2,1,0:T(8,128)S(1)} fusion(f32[160,10,256]{2,0,1:T(8,128)} %reshape.236, f32[80,160]{1,0:T(8,128)S(1)} %collective-permute-done.2, f32[80,160]{1,0:T(8,128)S(1)} %maximum_select_fusion.1, pred[]{:T(512)S(6)} %eq.114), kind=kOutput, calls=%fused_computation.14 | convolution fusion | flops 786508800 | bytes 3379201 | tf_op jit(solution)/shard_map/ac,cbj->baj/dot_general | solution.py:92
  218.0 1.6 convolution_bitcast_fusion
  219.6 1.9 pad_maximum_fusion
  (22 shorter events, 0.9 us)
Async XLA Ops:
  6.8 20.5 %all-to-all-start = ((s32[8,1,8]{2,1,0:T(1,128)}), s32[8,1,8]{2,1,0:T(1,128)S(1)}, u32[]{:S(2)}, u32[]{:S(2)}) async-start(s32[8,1,8]{2,1,0:T(1,128)} %bitcast.6), calls=%async_computation | async-start | bytes 8192 | tf_op jit(solution)/shard_map/all_to_all | solution.py:72
  27.4 6.1 %copy-start.1 = (f32[20,160]{1,0:T(8,128)S(1)}, f32[20,160]{1,0:T(8,128)}, u32[]{:S(2)}) copy-start(f32[20,160]{1,0:T(8,128)} %param.12) | copy-start | bytes 38404
  27.4 152.0 %all-to-all-start.1 = ((f32[8,8,25600]{2,1,0:T(8,128)}), f32[8,8,25600]{2,1,0:T(8,128)}, u32[]{:S(2)}, u32[]{:S(2)}) async-start(f32[8,8,25600]{2,1,0:T(8,128)} %fusion.12), calls=%async_computation.1 | async-start | bytes 13107200 | tf_op jit(solution)/shard_map/all_to_all | solution.py:71
  33.5 53.0 %collective-permute-start = (f32[20,160]{1,0:T(8,128)S(1)}, f32[20,160]{1,0:T(8,128)S(1)}, u32[]{:S(2)}, u32[]{:S(2)}) collective-permute-start(f32[20,160]{1,0:T(8,128)S(1)} %copy-done.1), channel_id=1, source_target_pairs={{0,4},{4,0},{8,12},{12,8},{16,20},{20,16},{24,28},{28,24},{1,5},{5... | collective-permute-start | bytes 38408 | tf_op jit(solution)/shard_map/ppermute | solution.py:14
  86.5 53.7 %collective-permute-start.1 = (f32[40,160]{1,0:T(8,128)S(1)}, f32[40,160]{1,0:T(8,128)S(1)}, u32[]{:S(2)}, u32[]{:S(2)}) collective-permute-start(f32[40,160]{1,0:T(8,128)S(1)} %maximum_select_fusion.2), channel_id=1, source_target_pairs={{0,8},{4,12},{8,0},{12,4},{16,24},{20,28},{24,16},{28,20},{1,9},{5... | collective-permute-start | bytes 76808 | tf_op jit(solution)/shard_map/ppermute | solution.py:14
  140.2 74.6 %collective-permute-start.2 = (f32[80,160]{1,0:T(8,128)S(1)}, f32[80,160]{1,0:T(8,128)S(1)}, u32[]{:S(2)}, u32[]{:S(2)}) collective-permute-start(f32[80,160]{1,0:T(8,128)S(1)} %maximum_select_fusion.1), channel_id=1, source_target_pairs={{0,16},{4,20},{8,24},{12,28},{16,0},{20,4},{24,8},{28,12},{1,17},{... | collective-permute-start | bytes 153608 | tf_op jit(solution)/shard_map/ppermute | solution.py:14
  214.8 3.2 %copy-start = (f32[160,10,256]{2,0,1:T(8,128)S(1)}, f32[160,10,256]{2,0,1:T(8,128)}, u32[]{:S(2)}) copy-start(f32[160,10,256]{2,0,1:T(8,128)} %reshape.237) | copy-start | bytes 4915204
